TPU v7x, 16 devices: a whole 2x2x2 slice. The times are simulated.
16 devices in a mesh: pp: 2 (over z), dp: 8 (over y, x, core).
Axes of the slice: x: 2, y: 2, z: 2, core: 2. Of those that a mesh axis runs over, the one named last changes fastest.
Arguments:
- x_in: bfloat16 [12, 48, 128, 768], P(None, 'dp')
- grad_y: bfloat16 [12, 48, 128, 768], P(None, 'dp')
- w_qkv: bfloat16 [2, 1, 768, 2304], P('pp')
- w_out: bfloat16 [2, 1, 768, 768], P('pp')
- w_up: bfloat16 [2, 1, 768, 3072], P('pp')
- w_down: bfloat16 [2, 1, 3072, 768], P('pp')
Outputs:
- output 1: float32 [2, 1, 768, 2304], P('pp', None, 'dp')
- output 2: float32 [2, 1, 768, 768], P('pp', None, 'dp')
- output 3: float32 [2, 1, 768, 3072], P('pp', None, 'dp')
- output 4: float32 [2, 1, 3072, 768], P('pp', None, 'dp')
- output 5: bfloat16 [12, 48, 128, 768], P(None, 'dp')
All inputs are finite; a program needn't handle non-finite values.
Results may differ from a plain program's by a relative error of at most 0.0188847.
Values are sent between devices in bfloat16 or wider.
A program may use at most 1 GiB of HBM per device.

v0:
```python
import jax
import jax.numpy as jnp
from jax import lax
from jax.sharding import PartitionSpec as P, NamedSharding

HEAD_DIM = 64
NORM_EPS = 1e-6


def rms_norm(hidden):
    wide_h = hidden.astype(jnp.float32)
    return wide_h * lax.rsqrt(jnp.mean(wide_h * wide_h, axis=-1, keepdims=True) + NORM_EPS)


def gelu_tanh(pre_act):
    return jax.nn.gelu(pre_act, approximate=True)


def layer_forward(hidden, w_qkv, w_out, w_up, w_down):
    batch_rows, seq_len, d_model = hidden.shape
    n_heads = d_model // HEAD_DIM
    normed = rms_norm(hidden).astype(jnp.bfloat16)
    qkv_act = jnp.einsum("bsd,dthe->tbshe", normed, w_qkv.reshape(d_model, 3, n_heads, HEAD_DIM), preferred_element_type=jnp.float32).astype(jnp.bfloat16)
    q_act = qkv_act[0]
    k_act = qkv_act[1]
    v_act = qkv_act[2]
    scores = jnp.einsum("bqhe,bkhe->bhqk", q_act, k_act, preferred_element_type=jnp.float32) * HEAD_DIM ** -0.5
    causal = lax.broadcasted_iota(jnp.int32, (seq_len, seq_len), 0) >= lax.broadcasted_iota(jnp.int32, (seq_len, seq_len), 1)
    attn_probs = jax.nn.softmax(jnp.where(causal, scores, -1e30), axis=-1).astype(jnp.bfloat16)
    attn_cat = jnp.einsum("bhqk,bkhe->bqhe", attn_probs, v_act, preferred_element_type=jnp.float32).astype(jnp.bfloat16).reshape(batch_rows, seq_len, d_model)
    resid_mid = (hidden.astype(jnp.float32) + jnp.einsum("bsd,de->bse", attn_cat, w_out, preferred_element_type=jnp.float32)).astype(jnp.bfloat16)
    normed_mid = rms_norm(resid_mid).astype(jnp.bfloat16)
    up_act = jnp.einsum("bsd,df->bsf", normed_mid, w_up, preferred_element_type=jnp.float32).astype(jnp.bfloat16)
    gelu_act = gelu_tanh(up_act.astype(jnp.float32)).astype(jnp.bfloat16)
    resid_out = (resid_mid.astype(jnp.float32) + jnp.einsum("bsf,fd->bsd", gelu_act, w_down, preferred_element_type=jnp.float32)).astype(jnp.bfloat16)
    return resid_out, (normed, q_act, k_act, v_act, attn_probs, attn_cat, resid_mid, normed_mid, up_act, gelu_act)


def layer_backward(kept_acts, hidden, grad_top, w_qkv, w_out, w_up, w_down):
    normed, q_act, k_act, v_act, attn_probs, attn_cat, resid_mid, normed_mid, up_act, gelu_act = kept_acts
    batch_rows, seq_len, d_model = hidden.shape
    n_heads = d_model // HEAD_DIM
    dw_down = jnp.einsum("bsf,bsd->fd", gelu_act, grad_top, preferred_element_type=jnp.float32)
    grad_gelu = jnp.einsum("bsd,fd->bsf", grad_top, w_down, preferred_element_type=jnp.float32)
    _, gelu_pull = jax.vjp(gelu_tanh, up_act.astype(jnp.float32))
    grad_up_act = gelu_pull(grad_gelu)[0].astype(jnp.bfloat16)
    dw_up = jnp.einsum("bsd,bsf->df", normed_mid, grad_up_act, preferred_element_type=jnp.float32)
    grad_nmid = jnp.einsum("bsf,df->bsd", grad_up_act, w_up, preferred_element_type=jnp.float32)
    _, norm_pull_mid = jax.vjp(rms_norm, resid_mid.astype(jnp.float32))
    grad_mid = (grad_top.astype(jnp.float32) + norm_pull_mid(grad_nmid)[0]).astype(jnp.bfloat16)
    dw_out = jnp.einsum("bsd,bse->de", attn_cat, grad_mid, preferred_element_type=jnp.float32)
    grad_cat = jnp.einsum("bse,de->bsd", grad_mid, w_out, preferred_element_type=jnp.float32).astype(jnp.bfloat16)
    grad_heads = grad_cat.reshape(batch_rows, seq_len, n_heads, HEAD_DIM)
    grad_probs = jnp.einsum("bqhe,bkhe->bhqk", grad_heads, v_act, preferred_element_type=jnp.float32)
    grad_v = jnp.einsum("bhqk,bqhe->bkhe", attn_probs, grad_heads, preferred_element_type=jnp.float32).astype(jnp.bfloat16)
    probs_wide = attn_probs.astype(jnp.float32)
    grad_scores = (probs_wide * (grad_probs - jnp.sum(grad_probs * probs_wide, axis=-1, keepdims=True)) * HEAD_DIM ** -0.5).astype(jnp.bfloat16)
    grad_q = jnp.einsum("bhqk,bkhe->bqhe", grad_scores, k_act, preferred_element_type=jnp.float32).astype(jnp.bfloat16)
    grad_k = jnp.einsum("bhqk,bqhe->bkhe", grad_scores, q_act, preferred_element_type=jnp.float32).astype(jnp.bfloat16)
    grad_qkv_act = jnp.stack([grad_q, grad_k, grad_v])
    dw_qkv = jnp.einsum("bsd,tbshe->dthe", normed, grad_qkv_act, preferred_element_type=jnp.float32).reshape(d_model, 3 * d_model)
    grad_normed = jnp.einsum("tbshe,dthe->bsd", grad_qkv_act, w_qkv.reshape(d_model, 3, n_heads, HEAD_DIM), preferred_element_type=jnp.float32)
    _, norm_pull_in = jax.vjp(rms_norm, hidden.astype(jnp.float32))
    grad_in = (grad_mid.astype(jnp.float32) + norm_pull_in(grad_normed)[0]).astype(jnp.bfloat16)
    return grad_in, (dw_qkv, dw_out, dw_up, dw_down)


def stage_forward(stage_weights, hidden):
    w_qkv, w_out, w_up, w_down = stage_weights
    for layer_idx in range(w_qkv.shape[0]):
        hidden, _ = layer_forward(hidden, w_qkv[layer_idx], w_out[layer_idx], w_up[layer_idx], w_down[layer_idx])
    return hidden


def stage_backward(stage_weights, hidden, grad_top):
    w_qkv, w_out, w_up, w_down = stage_weights
    n_layers = w_qkv.shape[0]
    layer_inputs = []
    kept_list = []
    for layer_idx in range(n_layers):
        layer_inputs.append(hidden)
        hidden, kept_acts = layer_forward(hidden, w_qkv[layer_idx], w_out[layer_idx], w_up[layer_idx], w_down[layer_idx])
        kept_list.append(kept_acts)
    grad_lists = ([], [], [], [])
    for layer_idx in reversed(range(n_layers)):
        grad_top, layer_grads = layer_backward(kept_list[layer_idx], layer_inputs[layer_idx], grad_top, w_qkv[layer_idx], w_out[layer_idx], w_up[layer_idx], w_down[layer_idx])
        for slot_idx in range(4):
            grad_lists[slot_idx].insert(0, layer_grads[slot_idx])
    return grad_top, tuple(jnp.stack(grad_list) for grad_list in grad_lists)


def schedule(tick_idx, stage_idx, n_stages, n_micro):
    warm_up = (tick_idx >= stage_idx) & (tick_idx < n_stages)
    steady_pos = tick_idx - (2 * n_stages - 1 - stage_idx)
    steady_on = steady_pos >= 0
    half_pos = steady_pos // 2
    is_back = steady_on & (steady_pos % 2 == 0) & (half_pos < n_micro)
    late_fwd = (tick_idx - stage_idx) // 2
    is_late = steady_on & (steady_pos % 2 == 1) & (late_fwd < n_micro)
    op_code = jnp.where(warm_up | is_late, 1, jnp.where(is_back, 2, 0))
    micro_idx = jnp.where(warm_up, tick_idx - stage_idx, jnp.where(is_late, late_fwd, jnp.where(is_back, half_pos, 0)))
    return op_code, micro_idx


def solution(mesh):
    n_stages = mesh.shape["pp"]
    fwd_pairs = [(src_idx, src_idx + 1) for src_idx in range(n_stages - 1)]
    bwd_pairs = [(src_idx + 1, src_idx) for src_idx in range(n_stages - 1)]

    def device_step(x_loc, g_loc, wqkv_loc, wout_loc, wup_loc, wdown_loc):
        stage_weights = (wqkv_loc[0], wout_loc[0], wup_loc[0], wdown_loc[0])
        n_micro = x_loc.shape[0]
        stage_idx = lax.axis_index("pp")
        is_last = stage_idx == n_stages - 1
        act_zeros = jnp.zeros(x_loc.shape[1:], jnp.bfloat16)

        def skip_op(micro_idx, stage_inputs, last_outputs, grad_accs, grad_recv):
            return act_zeros, act_zeros, last_outputs, grad_accs

        def forward_op(micro_idx, stage_inputs, last_outputs, grad_accs, grad_recv):
            hidden_out = stage_forward(stage_weights, lax.dynamic_index_in_dim(stage_inputs, micro_idx, 0, keepdims=False))
            new_outputs = lax.dynamic_update_index_in_dim(last_outputs, hidden_out, micro_idx, 0)
            return hidden_out, act_zeros, new_outputs, grad_accs

        def backward_op(micro_idx, stage_inputs, last_outputs, grad_accs, grad_recv):
            hidden_in = lax.dynamic_index_in_dim(stage_inputs, micro_idx, 0, keepdims=False)
            grad_top = jnp.where(is_last, lax.dynamic_index_in_dim(g_loc, micro_idx, 0, keepdims=False), grad_recv)
            grad_in, stage_grads = stage_backward(stage_weights, hidden_in, grad_top)
            new_accs = tuple(acc_part + new_part for acc_part, new_part in zip(grad_accs, stage_grads))
            return act_zeros, grad_in, last_outputs, new_accs

        def tick_body(tick_idx, loop_state):
            stage_inputs, last_outputs, grad_accs, grad_recv = loop_state
            op_code, micro_idx = schedule(tick_idx, stage_idx, n_stages, n_micro)
            send_fwd, send_bwd, last_outputs, grad_accs = lax.switch(op_code, (skip_op, forward_op, backward_op), micro_idx, stage_inputs, last_outputs, grad_accs, grad_recv)
            recv_fwd = lax.ppermute(send_fwd, "pp", fwd_pairs)
            recv_bwd = lax.ppermute(send_bwd, "pp", bwd_pairs)
            prev_code, prev_micro = schedule(tick_idx, stage_idx - 1, n_stages, n_micro)
            arrived = (stage_idx > 0) & (prev_code == 1)
            held_in = lax.dynamic_index_in_dim(stage_inputs, prev_micro, 0, keepdims=False)
            stage_inputs = lax.dynamic_update_index_in_dim(stage_inputs, jnp.where(arrived, recv_fwd, held_in), prev_micro, 0)
            return stage_inputs, last_outputs, grad_accs, recv_bwd

        init_accs = tuple(jnp.zeros(weight.shape, jnp.float32) for weight in stage_weights)
        init_state = (x_loc, jnp.zeros_like(x_loc), init_accs, act_zeros)
        loop_out = lax.fori_loop(0, 2 * (n_micro + n_stages - 1), tick_body, init_state)
        last_outputs = loop_out[1]
        grad_accs = loop_out[2]
        y_full = lax.psum(jnp.where(is_last, last_outputs, jnp.zeros_like(last_outputs)), "pp")
        grad_shards = tuple(lax.psum_scatter(acc_part, "dp", scatter_dimension=1, tiled=True)[None] for acc_part in grad_accs)
        return grad_shards + (y_full,)

    stage_spec = P("pp")
    shard_spec = P("pp", None, "dp", None)
    return jax.shard_map(device_step, mesh=mesh, in_specs=(P(None, "dp"), P(None, "dp"), stage_spec, stage_spec, stage_spec, stage_spec), out_specs=(shard_spec, shard_spec, shard_spec, shard_spec, P(None, "dp")), check_vma=False)
```

profile of v0, /device:TPU:0, one launch (start us, length us, event | category | flops | bytes accessed | tf_op | source)
XLA Modules:
  0.0 3709.3 jit_solution(9404477927407280183)
XLA Ops:
  43.6 3320.2 %while.28 = (s32[]{:T(128)}, bf16[12,6,128,768]{3,2,1,0:T(8,128)(2,1)}, bf16[12,6,128,768]{3,2,1,0:T(8,128)(2,1)}, f32[1,768,2304]{2,1,0:T(8,128)}, f32[1,768,76...) while((s32[]{:T(128)}, ...), condition=%wide.region_15.16_spmd, body=%wide.region_0.15_spmd.sunk | while | flops 30043910144 | bytes 540455360 | solution.py:146
  43.6 35.1 conditional.2
  82.9 23.4 collective-permute-done
  111.0 26.4 conditional.2
  150.1 22.6 collective-permute-done
  177.4 118.6 %collective-permute-start = (bf16[6,128,768]{2,1,0:T(8,128)(2,1)S(1)}, bf16[6,128,768]{2,1,0:T(8,128)(2,1)S(1)}, u32[]{:S(2)}, u32[]{:S(2)}) collective-permute-start(bf16[6,128,768]{2,1,0:T(8,128)(2,1)S(1)} %get-tuple-element.774), channel_id=1, source_target_pairs={{0,8},{1,9},{2,10},{3,11},{4,12},{5,13},{6,14},{7,15}} | collective-permute-start | bytes 3538952 | tf_op jit(solution)/shard_map/while/body/eval_jaxpr/ppermute | solution.py:136
  298.8 21.8 collective-permute-done
  324.8 106.1 %conditional.2 = (bf16[6,128,768]{2,1,0:T(8,128)(2,1)S(1)}, bf16[6,128,768]{2,1,0:T(8,128)(2,1)S(1)}, bf16[12,6,128,768]{3,2,1,0:T(8,128)(2,1)}, f32[1,768,2304]...) conditional(s32[]{:T(128)} %clamp.12, ...), branch_computations={%region_1.1_spmd, %region_2.6_spmd, %region_7.14_spmd} | conditional | flops 30043320320 | bytes 520399744 | solution.py:135
  435.1 20.9 collective-permute-done
  460.5 34.7 conditional.2
  495.2 73.0 %collective-permute-start = (bf16[6,128,768]{2,1,0:T(8,128)(2,1)S(1)}, bf16[6,128,768]{2,1,0:T(8,128)(2,1)S(1)}, u32[]{:S(2)}, u32[]{:S(2)}) collective-permute-start(bf16[6,128,768]{2,1,0:T(8,128)(2,1)S(1)} %get-tuple-element.774), channel_id=1, source_target_pairs={{0,8},{1,9},{2,10},{3,11},{4,12},{5,13},{6,14},{7,15}} | collective-permute-start | bytes 3538952 | tf_op jit(solution)/shard_map/while/body/eval_jaxpr/ppermute | solution.py:136
  570.9 20.1 collective-permute-done
  595.2 105.6 %conditional.2 = (bf16[6,128,768]{2,1,0:T(8,128)(2,1)S(1)}, bf16[6,128,768]{2,1,0:T(8,128)(2,1)S(1)}, bf16[12,6,128,768]{3,2,1,0:T(8,128)(2,1)}, f32[1,768,2304]...) conditional(s32[]{:T(128)} %clamp.12, ...), branch_computations={%region_1.1_spmd, %region_2.6_spmd, %region_7.14_spmd} | conditional | flops 30043320320 | bytes 520399744 | solution.py:135
  705.0 19.2 collective-permute-done
  728.8 35.0 conditional.2
  763.8 83.7 %collective-permute-start = (bf16[6,128,768]{2,1,0:T(8,128)(2,1)S(1)}, bf16[6,128,768]{2,1,0:T(8,128)(2,1)S(1)}, u32[]{:S(2)}, u32[]{:S(2)}) collective-permute-start(bf16[6,128,768]{2,1,0:T(8,128)(2,1)S(1)} %get-tuple-element.774), channel_id=1, source_target_pairs={{0,8},{1,9},{2,10},{3,11},{4,12},{5,13},{6,14},{7,15}} | collective-permute-start | bytes 3538952 | tf_op jit(solution)/shard_map/while/body/eval_jaxpr/ppermute | solution.py:136
  850.3 18.4 collective-permute-done
  873.2 110.2 %conditional.2 = (bf16[6,128,768]{2,1,0:T(8,128)(2,1)S(1)}, bf16[6,128,768]{2,1,0:T(8,128)(2,1)S(1)}, bf16[12,6,128,768]{3,2,1,0:T(8,128)(2,1)}, f32[1,768,2304]...) conditional(s32[]{:T(128)} %clamp.12, ...), branch_computations={%region_1.1_spmd, %region_2.6_spmd, %region_7.14_spmd} | conditional | flops 30043320320 | bytes 520399744 | solution.py:135
  987.6 17.5 collective-permute-done
  1009.6 34.7 conditional.2
  1044.3 73.0 %collective-permute-start = (bf16[6,128,768]{2,1,0:T(8,128)(2,1)S(1)}, bf16[6,128,768]{2,1,0:T(8,128)(2,1)S(1)}, u32[]{:S(2)}, u32[]{:S(2)}) collective-permute-start(bf16[6,128,768]{2,1,0:T(8,128)(2,1)S(1)} %get-tuple-element.774), channel_id=1, source_target_pairs={{0,8},{1,9},{2,10},{3,11},{4,12},{5,13},{6,14},{7,15}} | collective-permute-start | bytes 3538952 | tf_op jit(solution)/shard_map/while/body/eval_jaxpr/ppermute | solution.py:136
  1120.0 16.6 collective-permute-done
  1140.9 105.6 %conditional.2 = (bf16[6,128,768]{2,1,0:T(8,128)(2,1)S(1)}, bf16[6,128,768]{2,1,0:T(8,128)(2,1)S(1)}, bf16[12,6,128,768]{3,2,1,0:T(8,128)(2,1)}, f32[1,768,2304]...) conditional(s32[]{:T(128)} %clamp.12, ...), branch_computations={%region_1.1_spmd, %region_2.6_spmd, %region_7.14_spmd} | conditional | flops 30043320320 | bytes 520399744 | solution.py:135
  1250.7 15.8 collective-permute-done
  1271.1 35.0 conditional.2
  1306.1 83.7 %collective-permute-start = (bf16[6,128,768]{2,1,0:T(8,128)(2,1)S(1)}, bf16[6,128,768]{2,1,0:T(8,128)(2,1)S(1)}, u32[]{:S(2)}, u32[]{:S(2)}) collective-permute-start(bf16[6,128,768]{2,1,0:T(8,128)(2,1)S(1)} %get-tuple-element.774), channel_id=1, source_target_pairs={{0,8},{1,9},{2,10},{3,11},{4,12},{5,13},{6,14},{7,15}} | collective-permute-start | bytes 3538952 | tf_op jit(solution)/shard_map/while/body/eval_jaxpr/ppermute | solution.py:136
  1392.5 14.9 collective-permute-done
  1412.1 110.2 %conditional.2 = (bf16[6,128,768]{2,1,0:T(8,128)(2,1)S(1)}, bf16[6,128,768]{2,1,0:T(8,128)(2,1)S(1)}, bf16[12,6,128,768]{3,2,1,0:T(8,128)(2,1)}, f32[1,768,2304]...) conditional(s32[]{:T(128)} %clamp.12, ...), branch_computations={%region_1.1_spmd, %region_2.6_spmd, %region_7.14_spmd} | conditional | flops 30043320320 | bytes 520399744 | solution.py:135
  1526.5 14.1 collective-permute-done
  1545.0 34.7 conditional.2
  1579.8 73.0 %collective-permute-start = (bf16[6,128,768]{2,1,0:T(8,128)(2,1)S(1)}, bf16[6,128,768]{2,1,0:T(8,128)(2,1)S(1)}, u32[]{:S(2)}, u32[]{:S(2)}) collective-permute-start(bf16[6,128,768]{2,1,0:T(8,128)(2,1)S(1)} %get-tuple-element.774), channel_id=1, source_target_pairs={{0,8},{1,9},{2,10},{3,11},{4,12},{5,13},{6,14},{7,15}} | collective-permute-start | bytes 3538952 | tf_op jit(solution)/shard_map/while/body/eval_jaxpr/ppermute | solution.py:136
  1655.5 13.2 collective-permute-done
  1672.9 105.6 %conditional.2 = (bf16[6,128,768]{2,1,0:T(8,128)(2,1)S(1)}, bf16[6,128,768]{2,1,0:T(8,128)(2,1)S(1)}, bf16[12,6,128,768]{3,2,1,0:T(8,128)(2,1)}, f32[1,768,2304]...) conditional(s32[]{:T(128)} %clamp.12, ...), branch_computations={%region_1.1_spmd, %region_2.6_spmd, %region_7.14_spmd} | conditional | flops 30043320320 | bytes 520399744 | solution.py:135
  1782.7 12.4 collective-permute-done
  1799.7 35.0 conditional.2
  1834.7 83.7 %collective-permute-start = (bf16[6,128,768]{2,1,0:T(8,128)(2,1)S(1)}, bf16[6,128,768]{2,1,0:T(8,128)(2,1)S(1)}, u32[]{:S(2)}, u32[]{:S(2)}) collective-permute-start(bf16[6,128,768]{2,1,0:T(8,128)(2,1)S(1)} %get-tuple-element.774), channel_id=1, source_target_pairs={{0,8},{1,9},{2,10},{3,11},{4,12},{5,13},{6,14},{7,15}} | collective-permute-start | bytes 3538952 | tf_op jit(solution)/shard_map/while/body/eval_jaxpr/ppermute | solution.py:136
  1921.2 11.5 collective-permute-done
  1937.3 110.2 %conditional.2 = (bf16[6,128,768]{2,1,0:T(8,128)(2,1)S(1)}, bf16[6,128,768]{2,1,0:T(8,128)(2,1)S(1)}, bf16[12,6,128,768]{3,2,1,0:T(8,128)(2,1)}, f32[1,768,2304]...) conditional(s32[]{:T(128)} %clamp.12, ...), branch_computations={%region_1.1_spmd, %region_2.6_spmd, %region_7.14_spmd} | conditional | flops 30043320320 | bytes 520399744 | solution.py:135
  2051.7 10.8 collective-permute-done
  2067.3 34.7 conditional.2
  2102.0 72.9 %collective-permute-start = (bf16[6,128,768]{2,1,0:T(8,128)(2,1)S(1)}, bf16[6,128,768]{2,1,0:T(8,128)(2,1)S(1)}, u32[]{:S(2)}, u32[]{:S(2)}) collective-permute-start(bf16[6,128,768]{2,1,0:T(8,128)(2,1)S(1)} %get-tuple-element.774), channel_id=1, source_target_pairs={{0,8},{1,9},{2,10},{3,11},{4,12},{5,13},{6,14},{7,15}} | collective-permute-start | bytes 3538952 | tf_op jit(solution)/shard_map/while/body/eval_jaxpr/ppermute | solution.py:136
  2177.7 10.8 collective-permute-done
  2193.0 105.6 %conditional.2 = (bf16[6,128,768]{2,1,0:T(8,128)(2,1)S(1)}, bf16[6,128,768]{2,1,0:T(8,128)(2,1)S(1)}, bf16[12,6,128,768]{3,2,1,0:T(8,128)(2,1)}, f32[1,768,2304]...) conditional(s32[]{:T(128)} %clamp.12, ...), branch_computations={%region_1.1_spmd, %region_2.6_spmd, %region_7.14_spmd} | conditional | flops 30043320320 | bytes 520399744 | solution.py:135
  2302.8 10.8 collective-permute-done
  2318.6 35.0 conditional.2
  2353.6 83.6 %collective-permute-start = (bf16[6,128,768]{2,1,0:T(8,128)(2,1)S(1)}, bf16[6,128,768]{2,1,0:T(8,128)(2,1)S(1)}, u32[]{:S(2)}, u32[]{:S(2)}) collective-permute-start(bf16[6,128,768]{2,1,0:T(8,128)(2,1)S(1)} %get-tuple-element.774), channel_id=1, source_target_pairs={{0,8},{1,9},{2,10},{3,11},{4,12},{5,13},{6,14},{7,15}} | collective-permute-start | bytes 3538952 | tf_op jit(solution)/shard_map/while/body/eval_jaxpr/ppermute | solution.py:136
  2439.9 10.8 collective-permute-done
  2455.7 110.2 %conditional.2 = (bf16[6,128,768]{2,1,0:T(8,128)(2,1)S(1)}, bf16[6,128,768]{2,1,0:T(8,128)(2,1)S(1)}, bf16[12,6,128,768]{3,2,1,0:T(8,128)(2,1)}, f32[1,768,2304]...) conditional(s32[]{:T(128)} %clamp.12, ...), branch_computations={%region_1.1_spmd, %region_2.6_spmd, %region_7.14_spmd} | conditional | flops 30043320320 | bytes 520399744 | solution.py:135
  2570.0 10.8 collective-permute-done
  2585.6 34.7 conditional.2
  2620.3 72.9 %collective-permute-start = (bf16[6,128,768]{2,1,0:T(8,128)(2,1)S(1)}, bf16[6,128,768]{2,1,0:T(8,128)(2,1)S(1)}, u32[]{:S(2)}, u32[]{:S(2)}) collective-permute-start(bf16[6,128,768]{2,1,0:T(8,128)(2,1)S(1)} %get-tuple-element.774), channel_id=1, source_target_pairs={{0,8},{1,9},{2,10},{3,11},{4,12},{5,13},{6,14},{7,15}} | collective-permute-start | bytes 3538952 | tf_op jit(solution)/shard_map/while/body/eval_jaxpr/ppermute | solution.py:136
  2696.0 10.8 collective-permute-done
  2711.3 105.6 %conditional.2 = (bf16[6,128,768]{2,1,0:T(8,128)(2,1)S(1)}, bf16[6,128,768]{2,1,0:T(8,128)(2,1)S(1)}, bf16[12,6,128,768]{3,2,1,0:T(8,128)(2,1)}, f32[1,768,2304]...) conditional(s32[]{:T(128)} %clamp.12, ...), branch_computations={%region_1.1_spmd, %region_2.6_spmd, %region_7.14_spmd} | conditional | flops 30043320320 | bytes 520399744 | solution.py:135
  2821.1 10.8 collective-permute-done
  2836.9 35.0 conditional.2
  2871.9 83.6 %collective-permute-start = (bf16[6,128,768]{2,1,0:T(8,128)(2,1)S(1)}, bf16[6,128,768]{2,1,0:T(8,128)(2,1)S(1)}, u32[]{:S(2)}, u32[]{:S(2)}) collective-permute-start(bf16[6,128,768]{2,1,0:T(8,128)(2,1)S(1)} %get-tuple-element.774), channel_id=1, source_target_pairs={{0,8},{1,9},{2,10},{3,11},{4,12},{5,13},{6,14},{7,15}} | collective-permute-start | bytes 3538952 | tf_op jit(solution)/shard_map/while/body/eval_jaxpr/ppermute | solution.py:136
  2974.0 110.2 %conditional.2 = (bf16[6,128,768]{2,1,0:T(8,128)(2,1)S(1)}, bf16[6,128,768]{2,1,0:T(8,128)(2,1)S(1)}, bf16[12,6,128,768]{3,2,1,0:T(8,128)(2,1)}, f32[1,768,2304]...) conditional(s32[]{:T(128)} %clamp.12, ...), branch_computations={%region_1.1_spmd, %region_2.6_spmd, %region_7.14_spmd} | conditional | flops 30043320320 | bytes 520399744 | solution.py:135
  3109.4 102.1 %collective-permute-start = (bf16[6,128,768]{2,1,0:T(8,128)(2,1)S(1)}, bf16[6,128,768]{2,1,0:T(8,128)(2,1)S(1)}, u32[]{:S(2)}, u32[]{:S(2)}) collective-permute-start(bf16[6,128,768]{2,1,0:T(8,128)(2,1)S(1)} %get-tuple-element.774), channel_id=1, source_target_pairs={{0,8},{1,9},{2,10},{3,11},{4,12},{5,13},{6,14},{7,15}} | collective-permute-start | bytes 3538952 | tf_op jit(solution)/shard_map/while/body/eval_jaxpr/ppermute | solution.py:136
  3229.7 113.1 %conditional.2 = (bf16[6,128,768]{2,1,0:T(8,128)(2,1)S(1)}, bf16[6,128,768]{2,1,0:T(8,128)(2,1)S(1)}, bf16[12,6,128,768]{3,2,1,0:T(8,128)(2,1)}, f32[1,768,2304]...) conditional(s32[]{:T(128)} %clamp.12, ...), branch_computations={%region_1.1_spmd, %region_2.6_spmd, %region_7.14_spmd} | conditional | flops 30043320320 | bytes 520399744 | solution.py:135
  3371.3 27.0 reduce-scatter.7.cloned.1.call-done
  3398.3 63.2 %reduce-scatter.5.cloned.1.call-done = f32[1,96,2304]{2,1,0:T(8,128)} async-done(((f32[1,768,2304]{2,1,0:T(8,128)}), f32[1,96,2304]{2,1,0:T(8,128)}) %reduce-scatter.5.cloned.1.call-update) | async-done | bytes 884752 | tf_op jit(solution)/shard_map/reduce_scatter | solution.py:150
  3461.5 74.2 %reduce-scatter.9.cloned.1.call-done = f32[1,96,3072]{2,1,0:T(8,128)} async-done(((f32[1,768,3072]{2,1,0:T(8,128)}), f32[1,96,3072]{2,1,0:T(8,128)}) %reduce-scatter.9.cloned.1.call-update) | async-done | bytes 1179664 | tf_op jit(solution)/shard_map/reduce_scatter | solution.py:150
  3535.7 74.1 %reduce-scatter.11.cloned.1.call-done = f32[1,384,768]{2,1,0:T(8,128)} async-done(((f32[1,3072,768]{2,1,0:T(8,128)}), f32[1,384,768]{2,1,0:T(8,128)}) %reduce-scatter.11.cloned.1.call-update) | async-done | bytes 1179664 | tf_op jit(solution)/shard_map/reduce_scatter | solution.py:150
  3609.7 81.6 %all-reduce.2.cloned.1.call-done = bf16[12,6,128,768]{3,2,1,0:T(8,128)(2,1)} async-done(((bf16[12,6,128,768]{3,2,1,0:T(8,128)(2,1)}), bf16[12,6,128,768]{3,2,1,0:T(8,128)(2,1)}) %all-reduce.2.cloned.1.call-update) | async-done | bytes 14155792 | tf_op jit(solution)/shard_map/psum | solution.py:149
  (1522 shorter events, 1862.2 us)
Async XLA Ops:
  8.0 3390.3 %reduce-scatter.7.cloned.1.call-start = ((), (), s32[]{:S(2)}) async-start(), calls=%async_computation.5 | async-start | bytes 2654208 | tf_op jit(solution)/shard_map/reduce_scatter | solution.py:150
  78.7 27.6 collective-permute-start
  80.1 30.5 collective-permute-start.1
  137.4 35.3 collective-permute-start
  147.4 29.6 collective-permute-start.1
  177.4 118.6 %copy-start.9 = (bf16[6,128,768]{2,1,0:T(8,128)(2,1)}, bf16[6,128,768]{2,1,0:T(8,128)(2,1)S(1)}, u32[]{:S(2)}) copy-start(bf16[6,128,768]{2,1,0:T(8,128)(2,1)S(1)} %get-tuple-element.780) | copy-start | bytes 3538948 | tf_op jit(solution)/shard_map/while
  177.4 143.2 %collective-permute-start = (bf16[6,128,768]{2,1,0:T(8,128)(2,1)S(1)}, bf16[6,128,768]{2,1,0:T(8,128)(2,1)S(1)}, u32[]{:S(2)}, u32[]{:S(2)}) collective-permute-start(bf16[6,128,768]{2,1,0:T(8,128)(2,1)S(1)} %get-tuple-element.774), channel_id=1, source_target_pairs={{0,8},{1,9},{2,10},{3,11},{4,12},{5,13},{6,14},{7,15}} | collective-permute-start | bytes 3538952 | tf_op jit(solution)/shard_map/while/body/eval_jaxpr/ppermute | solution.py:136
  296.1 28.7 collective-permute-start.1
  431.0 25.0 collective-permute-start
  432.3 27.9 collective-permute-start.1
  495.2 95.8 %collective-permute-start = (bf16[6,128,768]{2,1,0:T(8,128)(2,1)S(1)}, bf16[6,128,768]{2,1,0:T(8,128)(2,1)S(1)}, u32[]{:S(2)}, u32[]{:S(2)}) collective-permute-start(bf16[6,128,768]{2,1,0:T(8,128)(2,1)S(1)} %get-tuple-element.774), channel_id=1, source_target_pairs={{0,8},{1,9},{2,10},{3,11},{4,12},{5,13},{6,14},{7,15}} | collective-permute-start | bytes 3538952 | tf_op jit(solution)/shard_map/while/body/eval_jaxpr/ppermute | solution.py:136
  568.2 27.0 collective-permute-start.1
  700.9 23.3 collective-permute-start
  702.2 26.2 collective-permute-start.1
  763.8 83.7 %copy-start.9 = (bf16[6,128,768]{2,1,0:T(8,128)(2,1)}, bf16[6,128,768]{2,1,0:T(8,128)(2,1)S(1)}, u32[]{:S(2)}) copy-start(bf16[6,128,768]{2,1,0:T(8,128)(2,1)S(1)} %get-tuple-element.780) | copy-start | bytes 3538948 | tf_op jit(solution)/shard_map/while
  763.8 104.8 %collective-permute-start = (bf16[6,128,768]{2,1,0:T(8,128)(2,1)S(1)}, bf16[6,128,768]{2,1,0:T(8,128)(2,1)S(1)}, u32[]{:S(2)}, u32[]{:S(2)}) collective-permute-start(bf16[6,128,768]{2,1,0:T(8,128)(2,1)S(1)} %get-tuple-element.774), channel_id=1, source_target_pairs={{0,8},{1,9},{2,10},{3,11},{4,12},{5,13},{6,14},{7,15}} | collective-permute-start | bytes 3538952 | tf_op jit(solution)/shard_map/while/body/eval_jaxpr/ppermute | solution.py:136
  847.5 25.3 collective-permute-start.1
  983.5 21.6 collective-permute-start
  984.9 24.5 collective-permute-start.1
  1044.3 92.4 %collective-permute-start = (bf16[6,128,768]{2,1,0:T(8,128)(2,1)S(1)}, bf16[6,128,768]{2,1,0:T(8,128)(2,1)S(1)}, u32[]{:S(2)}, u32[]{:S(2)}) collective-permute-start(bf16[6,128,768]{2,1,0:T(8,128)(2,1)S(1)} %get-tuple-element.774), channel_id=1, source_target_pairs={{0,8},{1,9},{2,10},{3,11},{4,12},{5,13},{6,14},{7,15}} | collective-permute-start | bytes 3538952 | tf_op jit(solution)/shard_map/while/body/eval_jaxpr/ppermute | solution.py:136
  1117.3 23.6 collective-permute-start.1
  1246.6 19.9 collective-permute-start
  1248.0 22.7 collective-permute-start.1
  1306.1 83.7 %copy-start.9 = (bf16[6,128,768]{2,1,0:T(8,128)(2,1)}, bf16[6,128,768]{2,1,0:T(8,128)(2,1)S(1)}, u32[]{:S(2)}) copy-start(bf16[6,128,768]{2,1,0:T(8,128)(2,1)S(1)} %get-tuple-element.780) | copy-start | bytes 3538948 | tf_op jit(solution)/shard_map/while
  1306.1 101.4 %collective-permute-start = (bf16[6,128,768]{2,1,0:T(8,128)(2,1)S(1)}, bf16[6,128,768]{2,1,0:T(8,128)(2,1)S(1)}, u32[]{:S(2)}, u32[]{:S(2)}) collective-permute-start(bf16[6,128,768]{2,1,0:T(8,128)(2,1)S(1)} %get-tuple-element.774), channel_id=1, source_target_pairs={{0,8},{1,9},{2,10},{3,11},{4,12},{5,13},{6,14},{7,15}} | collective-permute-start | bytes 3538952 | tf_op jit(solution)/shard_map/while/body/eval_jaxpr/ppermute | solution.py:136
  1389.8 21.9 collective-permute-start.1
  1522.4 18.2 collective-permute-start
  1523.8 21.0 collective-permute-start.1
  1579.8 89.0 %collective-permute-start = (bf16[6,128,768]{2,1,0:T(8,128)(2,1)S(1)}, bf16[6,128,768]{2,1,0:T(8,128)(2,1)S(1)}, u32[]{:S(2)}, u32[]{:S(2)}) collective-permute-start(bf16[6,128,768]{2,1,0:T(8,128)(2,1)S(1)} %get-tuple-element.774), channel_id=1, source_target_pairs={{0,8},{1,9},{2,10},{3,11},{4,12},{5,13},{6,14},{7,15}} | collective-permute-start | bytes 3538952 | tf_op jit(solution)/shard_map/while/body/eval_jaxpr/ppermute | solution.py:136
  1652.7 20.2 collective-permute-start.1
  1778.6 16.5 collective-permute-start
  1780.0 19.3 collective-permute-start.1
  1834.7 83.7 %copy-start.9 = (bf16[6,128,768]{2,1,0:T(8,128)(2,1)}, bf16[6,128,768]{2,1,0:T(8,128)(2,1)S(1)}, u32[]{:S(2)}) copy-start(bf16[6,128,768]{2,1,0:T(8,128)(2,1)S(1)} %get-tuple-element.780) | copy-start | bytes 3538948 | tf_op jit(solution)/shard_map/while
  1834.7 98.0 %collective-permute-start = (bf16[6,128,768]{2,1,0:T(8,128)(2,1)S(1)}, bf16[6,128,768]{2,1,0:T(8,128)(2,1)S(1)}, u32[]{:S(2)}, u32[]{:S(2)}) collective-permute-start(bf16[6,128,768]{2,1,0:T(8,128)(2,1)S(1)} %get-tuple-element.774), channel_id=1, source_target_pairs={{0,8},{1,9},{2,10},{3,11},{4,12},{5,13},{6,14},{7,15}} | collective-permute-start | bytes 3538952 | tf_op jit(solution)/shard_map/while/body/eval_jaxpr/ppermute | solution.py:136
  1918.4 18.5 collective-permute-start.1
  2047.6 15.0 collective-permute-start
  2048.9 18.1 collective-permute-start.1
  2102.0 86.5 %collective-permute-start = (bf16[6,128,768]{2,1,0:T(8,128)(2,1)S(1)}, bf16[6,128,768]{2,1,0:T(8,128)(2,1)S(1)}, u32[]{:S(2)}, u32[]{:S(2)}) collective-permute-start(bf16[6,128,768]{2,1,0:T(8,128)(2,1)S(1)} %get-tuple-element.774), channel_id=1, source_target_pairs={{0,8},{1,9},{2,10},{3,11},{4,12},{5,13},{6,14},{7,15}} | collective-permute-start | bytes 3538952 | tf_op jit(solution)/shard_map/while/body/eval_jaxpr/ppermute | solution.py:136
  2174.9 18.1 collective-permute-start.1
  2298.7 15.0 collective-permute-start
  2300.0 18.1 collective-permute-start.1
  2353.5 83.6 %copy-start.9 = (bf16[6,128,768]{2,1,0:T(8,128)(2,1)}, bf16[6,128,768]{2,1,0:T(8,128)(2,1)S(1)}, u32[]{:S(2)}) copy-start(bf16[6,128,768]{2,1,0:T(8,128)(2,1)S(1)} %get-tuple-element.780) | copy-start | bytes 3538948 | tf_op jit(solution)/shard_map/while
  2353.6 97.2 %collective-permute-start = (bf16[6,128,768]{2,1,0:T(8,128)(2,1)S(1)}, bf16[6,128,768]{2,1,0:T(8,128)(2,1)S(1)}, u32[]{:S(2)}, u32[]{:S(2)}) collective-permute-start(bf16[6,128,768]{2,1,0:T(8,128)(2,1)S(1)} %get-tuple-element.774), channel_id=1, source_target_pairs={{0,8},{1,9},{2,10},{3,11},{4,12},{5,13},{6,14},{7,15}} | collective-permute-start | bytes 3538952 | tf_op jit(solution)/shard_map/while/body/eval_jaxpr/ppermute | solution.py:136
  2437.1 18.1 collective-permute-start.1
  2565.9 15.0 collective-permute-start
  2567.3 18.1 collective-permute-start.1
  2620.3 86.5 %collective-permute-start = (bf16[6,128,768]{2,1,0:T(8,128)(2,1)S(1)}, bf16[6,128,768]{2,1,0:T(8,128)(2,1)S(1)}, u32[]{:S(2)}, u32[]{:S(2)}) collective-permute-start(bf16[6,128,768]{2,1,0:T(8,128)(2,1)S(1)} %get-tuple-element.774), channel_id=1, source_target_pairs={{0,8},{1,9},{2,10},{3,11},{4,12},{5,13},{6,14},{7,15}} | collective-permute-start | bytes 3538952 | tf_op jit(solution)/shard_map/while/body/eval_jaxpr/ppermute | solution.py:136
  2693.2 18.1 collective-permute-start.1
  2817.0 15.0 collective-permute-start
  2818.4 18.1 collective-permute-start.1
  2871.9 83.6 %copy-start.9 = (bf16[6,128,768]{2,1,0:T(8,128)(2,1)}, bf16[6,128,768]{2,1,0:T(8,128)(2,1)S(1)}, u32[]{:S(2)}) copy-start(bf16[6,128,768]{2,1,0:T(8,128)(2,1)S(1)} %get-tuple-element.780) | copy-start | bytes 3538948 | tf_op jit(solution)/shard_map/while
  2871.9 97.2 %collective-permute-start = (bf16[6,128,768]{2,1,0:T(8,128)(2,1)S(1)}, bf16[6,128,768]{2,1,0:T(8,128)(2,1)S(1)}, u32[]{:S(2)}, u32[]{:S(2)}) collective-permute-start(bf16[6,128,768]{2,1,0:T(8,128)(2,1)S(1)} %get-tuple-element.774), channel_id=1, source_target_pairs={{0,8},{1,9},{2,10},{3,11},{4,12},{5,13},{6,14},{7,15}} | collective-permute-start | bytes 3538952 | tf_op jit(solution)/shard_map/while/body/eval_jaxpr/ppermute | solution.py:136
  2955.5 18.1 collective-permute-start.1
  3084.2 15.0 collective-permute-start
  3085.6 18.1 collective-permute-start.1
  3109.4 102.1 %copy-start.9 = (bf16[6,128,768]{2,1,0:T(8,128)(2,1)}, bf16[6,128,768]{2,1,0:T(8,128)(2,1)S(1)}, u32[]{:S(2)}) copy-start(bf16[6,128,768]{2,1,0:T(8,128)(2,1)S(1)} %get-tuple-element.780) | copy-start | bytes 3538948 | tf_op jit(solution)/shard_map/while
  3109.4 115.7 %collective-permute-start = (bf16[6,128,768]{2,1,0:T(8,128)(2,1)S(1)}, bf16[6,128,768]{2,1,0:T(8,128)(2,1)S(1)}, u32[]{:S(2)}, u32[]{:S(2)}) collective-permute-start(bf16[6,128,768]{2,1,0:T(8,128)(2,1)S(1)} %get-tuple-element.774), channel_id=1, source_target_pairs={{0,8},{1,9},{2,10},{3,11},{4,12},{5,13},{6,14},{7,15}} | collective-permute-start | bytes 3538952 | tf_op jit(solution)/shard_map/while/body/eval_jaxpr/ppermute | solution.py:136
  3211.6 18.1 collective-permute-start.1
  3342.7 15.0 collective-permute-start
  3344.1 18.1 collective-permute-start.1
  3363.8 97.6 %reduce-scatter.5.cloned.1.call-start = ((), (), s32[]{:S(2)}) async-start(), calls=%async_computation.4 | async-start | bytes 7962624 | tf_op jit(solution)/shard_map/reduce_scatter | solution.py:150
  3364.6 171.1 %reduce-scatter.9.cloned.1.call-start = ((), (), s32[]{:S(2)}) async-start(), calls=%async_computation.6 | async-start | bytes 10616832 | tf_op jit(solution)/shard_map/reduce_scatter | solution.py:150
  3365.3 244.4 %reduce-scatter.11.cloned.1.call-start = ((), (), s32[]{:S(2)}) async-start(), calls=%async_computation.7 | async-start | bytes 10616832 | tf_op jit(solution)/shard_map/reduce_scatter | solution.py:150
  3365.9 325.5 %all-reduce.2.cloned.1.call-start = ((), (), s32[]{:S(2)}) async-start(), calls=%async_computation.8 | async-start | bytes 28311552 | tf_op jit(solution)/shard_map/psum | solution.py:149
  (380 other events, 2628.6 us)
Sparse Core Ops, SparseCore 0:
  3364.0 34.2 reduce-scatter.6
  3402.3 59.1 reduce-scatter.4
  3465.5 70.1 reduce-scatter.8
  3539.6 70.1 reduce-scatter.10
Sparse Core Ops, SparseCore 1:
  3371.4 319.9 all-reduce.1
where the time goes:
time: 3720 us; the launch traced here: 3710 us
  matrix products  1300 us (35%)
  starting transfers between devices  1070 us (29%)
  waiting for transfers between devices  782 us (21%)
  local copies, waits for them, and re-layouts  195 us (5%)
  other arithmetic  176 us (5%)
  loops' own time  175 us (5%)
    ppermute x26, starting transfers between devices, tick_body(): recv_fwd = lax.ppermute(send_fwd, 'pp', fwd_pairs)  1030 us
    ppermute x26, waiting for transfers between devices, tick_body(): recv_fwd = lax.ppermute(send_fwd, 'pp', fwd_pairs)  382 us
    reduce_scatter x4, waiting for transfers between devices, device_step(): lax.psum_scatter(acc_part, 'dp', scatter_dimension=1, tiled=True)[None]  238 us
    another operation x26, loops' own time, tick_body(): lax.switch(op_code, (skip_op, forward_op, backward_op), micro_idx, stage_...  164 us
    dot_general x24, matrix products, layer_forward(): jnp.einsum('bsd,dthe->tbshe', normed, w_qkv.reshape(d_model, 3, n_heads,...  140 us
    dot_general x12, matrix products, layer_backward(): jnp.einsum('bsd,bsf->df', normed_mid, grad_up_act, preferred_element_type...  126 us
    dot_general x12, matrix products, layer_backward(): jnp.einsum('bsf,bsd->fd', gelu_act, grad_top, preferred_element_type=jnp....  122 us
    dot_general x12, matrix products, layer_backward(): jnp.einsum('bsd,fd->bsf', grad_top, w_down, preferred_element_type=jnp.fl...  114 us
  transfers between devices with their start and end apart: 57, of which 57 were waited for; matrix products, arithmetic and copies ran while one was open for 2% of the time, Pallas kernels for 0%

commit v1 on v0

v1 whole, which is shorter than its diff:
```python
import functools

import jax
import jax.numpy as jnp
from jax import lax
from jax.experimental import pallas as pl
from jax.experimental.pallas import tpu as pltpu
from jax.sharding import PartitionSpec as P

HEAD_DIM = 64
PAIR = 2 * HEAD_DIM
NORM_EPS = 1e-6
ROWS_FWD = 2
ROWS_BWD = 2
EXP_SCALE = HEAD_DIM ** -0.5 * 1.4426950408889634
F32 = jnp.float32
BF16 = jnp.bfloat16
NEG = -1e30


def rms_norm(hidden):
    wide_h = hidden.astype(F32)
    return wide_h * lax.rsqrt(jnp.mean(wide_h * wide_h, axis=-1, keepdims=True) + NORM_EPS)


def gelu_tanh(pre_act):
    return jax.nn.gelu(pre_act, approximate=True)


def dot_nn(a, b):
    return lax.dot_general(a, b, (((1,), (0,)), ((), ())), preferred_element_type=F32)


def dot_nt(a, b):
    return lax.dot_general(a, b, (((1,), (1,)), ((), ())), preferred_element_type=F32)


def dot_tn(a, b):
    return lax.dot_general(a, b, (((0,), (0,)), ((), ())), preferred_element_type=F32)


def block_diag(pair, low):
    zero = jnp.zeros_like(pair)
    return jnp.concatenate([jnp.where(low, pair, zero), jnp.where(low, zero, pair)], axis=0)


def attn_fwd_kernel(qkv_ref, out_ref):
    rows, seq, width = qkv_ref.shape
    d_model = width // 3
    low = lax.broadcasted_iota(jnp.int32, (seq, PAIR), 1) < HEAD_DIM
    causal = lax.broadcasted_iota(jnp.int32, (seq, seq), 0) >= lax.broadcasted_iota(jnp.int32, (seq, seq), 1)
    for row in range(rows):
        for col in range(0, d_model, PAIR):
            q = qkv_ref[row, :, col:col + PAIR]
            k = block_diag(qkv_ref[row, :, d_model + col:d_model + col + PAIR], low)
            v = block_diag(qkv_ref[row, :, 2 * d_model + col:2 * d_model + col + PAIR], low)
            scores = dot_nt(q, k)
            probs = []
            for half in range(2):
                s = jnp.where(causal, scores[:, half * seq:(half + 1) * seq], NEG)
                e = jnp.exp2((s - jnp.max(s, axis=-1, keepdims=True)) * EXP_SCALE)
                probs.append((e * (1.0 / jnp.sum(e, axis=-1, keepdims=True))).astype(BF16))
            out_ref[row, :, col:col + PAIR] = dot_nn(jnp.concatenate(probs, axis=1), v).astype(BF16)


def attn_bwd_kernel(qkv_ref, do_ref, dqkv_ref):
    rows, seq, width = qkv_ref.shape
    d_model = width // 3
    low = lax.broadcasted_iota(jnp.int32, (seq, PAIR), 1) < HEAD_DIM
    causal = lax.broadcasted_iota(jnp.int32, (seq, seq), 0) <= lax.broadcasted_iota(jnp.int32, (seq, seq), 1)
    for row in range(rows):
        for col in range(0, d_model, PAIR):
            q = block_diag(qkv_ref[row, :, col:col + PAIR], low)
            k = qkv_ref[row, :, d_model + col:d_model + col + PAIR]
            v = qkv_ref[row, :, 2 * d_model + col:2 * d_model + col + PAIR]
            do = block_diag(do_ref[row, :, col:col + PAIR], low)
            scores = dot_nt(k, q)
            dprobs = dot_nt(v, do)
            probs, dscores = [], []
            for half in range(2):
                s = jnp.where(causal, scores[:, half * seq:(half + 1) * seq], NEG)
                e = jnp.exp2((s - jnp.max(s, axis=0, keepdims=True)) * EXP_SCALE)
                p = (e * (1.0 / jnp.sum(e, axis=0, keepdims=True))).astype(BF16)
                wide = p.astype(F32)
                dp = dprobs[:, half * seq:(half + 1) * seq]
                inner = jnp.sum(dp * wide, axis=0, keepdims=True)
                probs.append(p)
                dscores.append((wide * (dp - inner) * HEAD_DIM ** -0.5).astype(BF16))
            ds_wide = jnp.concatenate(dscores, axis=1)
            ds_tall = jnp.concatenate(dscores, axis=0)
            dqkv_ref[row, :, col:col + PAIR] = dot_tn(ds_tall, block_diag(k, low)).astype(BF16)
            dqkv_ref[row, :, d_model + col:d_model + col + PAIR] = dot_nn(ds_wide, q).astype(BF16)
            dqkv_ref[row, :, 2 * d_model + col:2 * d_model + col + PAIR] = dot_nn(jnp.concatenate(probs, axis=1), do).astype(BF16)


def attn_fwd(qkv, seq):
    tokens, width = qkv.shape
    rows = tokens // seq
    d_model = width // 3
    out = pl.pallas_call(
        attn_fwd_kernel,
        grid=(rows // ROWS_FWD,),
        in_specs=[pl.BlockSpec((ROWS_FWD, seq, width), lambda i: (i, 0, 0))],
        out_specs=pl.BlockSpec((ROWS_FWD, seq, d_model), lambda i: (i, 0, 0)),
        out_shape=jax.ShapeDtypeStruct((rows, seq, d_model), BF16),
        cost_estimate=pl.CostEstimate(flops=8 * tokens * seq * d_model, bytes_accessed=2 * tokens * 4 * d_model, transcendentals=0),
        name="attn_fwd",
    )(qkv.reshape(rows, seq, width))
    return out.reshape(tokens, d_model)


def attn_bwd(qkv, dout, seq):
    tokens, width = qkv.shape
    rows = tokens // seq
    d_model = width // 3
    out = pl.pallas_call(
        attn_bwd_kernel,
        grid=(rows // ROWS_BWD,),
        in_specs=[pl.BlockSpec((ROWS_BWD, seq, width), lambda i: (i, 0, 0)), pl.BlockSpec((ROWS_BWD, seq, d_model), lambda i: (i, 0, 0))],
        out_specs=pl.BlockSpec((ROWS_BWD, seq, width), lambda i: (i, 0, 0)),
        out_shape=jax.ShapeDtypeStruct((rows, seq, width), BF16),
        cost_estimate=pl.CostEstimate(flops=20 * tokens * seq * d_model, bytes_accessed=2 * tokens * 7 * d_model, transcendentals=0),
        name="attn_bwd",
    )(qkv.reshape(rows, seq, width), dout.reshape(rows, seq, d_model))
    return out.reshape(tokens, width)


def layer_forward(hidden, w_qkv, w_out, w_up, w_down, seq):
    normed = rms_norm(hidden).astype(BF16)
    qkv = dot_nn(normed, w_qkv).astype(BF16)
    cat = attn_fwd(qkv, seq)
    mid = (hidden.astype(F32) + dot_nn(cat, w_out)).astype(BF16)
    normed_mid = rms_norm(mid).astype(BF16)
    up = dot_nn(normed_mid, w_up).astype(BF16)
    gelu = gelu_tanh(up.astype(F32)).astype(BF16)
    out = (mid.astype(F32) + dot_nn(gelu, w_down)).astype(BF16)
    return out, (hidden, normed, qkv, cat, mid, normed_mid, up, gelu)


def layer_backward(kept, grad_top, w_qkv, w_out, w_up, w_down, seq, reduce_fn):
    hidden, normed, qkv, cat, mid, normed_mid, up, gelu = kept
    dw_down = reduce_fn(dot_tn(gelu, grad_top), 3)
    grad_gelu = dot_nt(grad_top, w_down)
    _, gelu_pull = jax.vjp(gelu_tanh, up.astype(F32))
    grad_up = gelu_pull(grad_gelu)[0].astype(BF16)
    dw_up = reduce_fn(dot_tn(normed_mid, grad_up), 2)
    grad_nmid = dot_nt(grad_up, w_up)
    _, norm_pull_mid = jax.vjp(rms_norm, mid.astype(F32))
    grad_mid = (grad_top.astype(F32) + norm_pull_mid(grad_nmid)[0]).astype(BF16)
    dw_out = reduce_fn(dot_tn(cat, grad_mid), 1)
    grad_cat = dot_nt(grad_mid, w_out).astype(BF16)
    grad_qkv = attn_bwd(qkv, grad_cat, seq)
    dw_qkv = reduce_fn(dot_tn(normed, grad_qkv), 0)
    grad_normed = dot_nt(grad_qkv, w_qkv)
    _, norm_pull_in = jax.vjp(rms_norm, hidden.astype(F32))
    grad_in = (grad_mid.astype(F32) + norm_pull_in(grad_normed)[0]).astype(BF16)
    return grad_in, (dw_qkv, dw_out, dw_up, dw_down)


def solution(mesh):
    n_stages = mesh.shape["pp"]
    n_rep = mesh.shape["dp"]

    def device_step(x_loc, g_loc, wqkv_loc, wout_loc, wup_loc, wdown_loc):
        n_micro, batch, seq, d_model = x_loc.shape
        stage_idx = lax.axis_index("pp")
        rep_idx = lax.axis_index("dp")
        is_first = stage_idx == 0
        share = n_micro // n_stages
        tokens = share * batch * seq

        def my_half(full):
            return lax.dynamic_slice_in_dim(full, stage_idx * share, share, 0).reshape(tokens, d_model)

        def gather_weight(w_loc):
            rows, cols = w_loc.shape[2:]
            piece = rows // n_rep
            mine = lax.dynamic_slice_in_dim(w_loc.reshape(rows, cols), rep_idx * piece, piece, 0)
            full = lax.all_gather(mine, ("pp", "dp"), axis=0, tiled=True)
            return [full[l * rows:(l + 1) * rows] for l in range(n_stages)]

        weights = list(zip(*[gather_weight(w) for w in (wqkv_loc, wout_loc, wup_loc, wdown_loc)]))

        def reduce_fn(dw, slot):
            return lax.psum_scatter(dw, "dp", scatter_dimension=0, tiled=True)

        hidden = my_half(x_loc)
        kept = []
        for l in range(n_stages):
            hidden, acts = layer_forward(hidden, *weights[l], seq)
            kept.append(acts)
        y_mine = hidden.reshape(share, batch, seq, d_model)
        y_peer = lax.ppermute(y_mine, "pp", [(0, 1), (1, 0)])
        y_full = jnp.where(is_first, jnp.concatenate([y_mine, y_peer]), jnp.concatenate([y_peer, y_mine]))

        grad = my_half(g_loc)
        shards = [None] * n_stages
        for l in reversed(range(n_stages)):
            grad, shards[l] = layer_backward(kept[l], grad, *weights[l], seq, reduce_fn)
        outs = []
        for slot in range(4):
            part = [shards[l][slot] for l in range(n_stages)]
            recv_1 = lax.ppermute(part[1], "pp", [(0, 1)])
            recv_0 = lax.ppermute(part[0], "pp", [(1, 0)])
            outs.append(jnp.where(is_first, part[0] + recv_0, part[1] + recv_1)[None, None])
        return tuple(outs) + (y_full,)

    stage_spec = P("pp")
    shard_spec = P("pp", None, "dp", None)
    return jax.shard_map(device_step, mesh=mesh, in_specs=(P(None, "dp"), P(None, "dp"), stage_spec, stage_spec, stage_spec, stage_spec), out_specs=(shard_spec, shard_spec, shard_spec, shard_spec, P(None, "dp")), check_vma=False)
```

time: 3720 us -> 1250 us (0.34)
  starting transfers between devices: 1070 us -> 26.7 us
  matrix products: 1300 us -> 650 us
  waiting for transfers between devices: 782 us -> 255 us
  Pallas kernels: 0 us -> 193 us
  loops' own time: 175 us -> 0 us
  local copies, waits for them, and re-layouts: 195 us -> 28 us
  other arithmetic: 176 us -> 74.8 us
    ppermute x52 -> x9, starting transfers between devices: 1060 us -> 26.2 us  [the longest x4 19.9 us: device_step(): recv_1 = lax.ppermute(part[1], 'pp', [(0, 1)])]
    dot_general x276 -> x23, matrix products: 1300 us -> 650 us  [the longest x7 236 us: dot_nt(): lax.dot_general(a, b, (((1,), (1,)), ((), ())), preferred_element_type=F32)]
    ppermute x52 -> x9, waiting for transfers between devices: 460 us -> 189 us  [the longest x4 177 us: device_step(): recv_1 = lax.ppermute(part[1], 'pp', [(0, 1)])]
    reduce_scatter x4 -> x8, waiting for transfers between devices: 238 us -> 0.05 us  [reduce_fn(): return lax.psum_scatter(dw, 'dp', scatter_dimension=0, tiled=True)]
    pallas_call x0 -> x4, Pallas kernels: none -> 193 us  [the longest x2 137 us: attn_bwd(): pl.pallas_call(attn_bwd_kernel, grid=(rows // ROWS_BWD,), in_specs=[pl.Bl...]
    another operation x27 -> x0, loops' own time: 175 us -> none  [the longest x26 164 us: tick_body(): lax.switch(op_code, (skip_op, forward_op, backward_op), micro_idx, stage_...]
    psum x1 -> x0, waiting for transfers between devices: 81.6 us -> none  [device_step(): lax.psum(jnp.where(is_last, last_outputs, jnp.zeros_like(last_outputs)),...]
    cond x720 -> x0, local copies, waits for them, and re-layouts: 78.5 us -> none
  transfers between devices with their start and end apart: 57 -> 21, of which waited for: 57 -> 9; matrix products, arithmetic and copies ran while one was open for 2% -> 42% of each run, Pallas kernels for 0% -> 13%
where the time goes in v1:
time: 1250 us; the launch traced here: 1240 us
  matrix products  650 us (52%)
  waiting for transfers between devices  255 us (20%)
  Pallas kernels  193 us (15%)
  other arithmetic  74.8 us (6%)
  local copies, waits for them, and re-layouts  28 us (2%)
  starting transfers between devices  26.7 us (2%)
  between operations  14.8 us (1%)
    dot_general x7, matrix products, dot_nt(): lax.dot_general(a, b, (((1,), (1,)), ((), ())), preferred_element_type=F32)  236 us
    dot_general x8, matrix products, dot_nn(): lax.dot_general(a, b, (((1,), (0,)), ((), ())), preferred_element_type=F32)  214 us
    dot_general x8, matrix products, dot_tn(): lax.dot_general(a, b, (((0,), (0,)), ((), ())), preferred_element_type=F32)  200 us
    ppermute x4, waiting for transfers between devices, device_step(): recv_1 = lax.ppermute(part[1], 'pp', [(0, 1)])  177 us
    pallas_call x2, Pallas kernels, attn_bwd(): pl.pallas_call(attn_bwd_kernel, grid=(rows // ROWS_BWD,), in_specs=[pl.Bl...  137 us
    all_gather x4, waiting for transfers between devices, gather_weight(): full = lax.all_gather(mine, ('pp', 'dp'), axis=0, tiled=True)  65.2 us
    pallas_call x2, Pallas kernels, attn_fwd(): pl.pallas_call(attn_fwd_kernel, grid=(rows // ROWS_FWD,), in_specs=[pl.Bl...  56.2 us
  transfers between devices with their start and end apart: 21, of which 9 were waited for; matrix products, arithmetic and copies ran while one was open for 42% of the time, Pallas kernels for 13%

profile of v1, /device:TPU:0, one launch (start us, length us, event | category | flops | bytes accessed | tf_op | source)
XLA Modules:
  0.0 1242.5 jit_solution(3757277408283417815)
XLA Ops:
  7.2 1.9 copy-done
  10.0 1.6 constant_dynamic-slice_fusion.1
  11.7 1.9 constant_dynamic-slice_fusion
  13.7 1.9 constant_dynamic-slice_fusion.2
  15.7 4.5 fusion.38
  20.2 6.7 constant_dynamic-slice_fusion.5
  26.9 6.6 constant_dynamic-slice_fusion.3
  33.5 7.2 fusion.40
  40.7 17.3 %all-gather.9.cloned.1.call-done = bf16[1,1,1536,2304]{3,2,1,0:T(8,128)(2,1)} async-done(((bf16[1,1,96,2304]{3,2,1,0:T(8,128)(2,1)}), bf16[1,1,1536,2304]{3,2,1,0:T(8,128)(2,1)}) %all-gather.9.cloned.1.call-update) | async-done | bytes 7077904 | tf_op jit(solution)/shard_map/all_gather | solution.py:179
  58.0 23.6 %convolution_convert_fusion.3 = bf16[4608,2304]{1,0:T(8,128)(2,1)} fusion(bf16[4608,768]{1,0:T(8,128)(2,1)} %fusion.40, bf16[1,1,1536,2304]{3,2,1,0:T(8,128)(2,1)} %all-gather.9.cloned.1.call-done), kind=kOutput, calls=%fused_computation.33 | convolution fusion | flops 16318070784 | bytes 31850496 | tf_op jit(solution)/shard_map/dot_general | solution.py:31
  81.6 28.0 %attn_fwd.2 = bf16[36,128,768]{2,1,0:T(8,128)(2,1)} custom-call(bf16[36,128,2304]{2,1,0:T(8,128)(2,1)} %bitcast.97), custom_call_target="tpu_custom_call" | custom-call | flops 3623878656 | bytes 28311552 | tf_op jit(solution)/shard_map/attn_fwd/pallas_call | solution.py:100
  109.6 11.8 fusion.26
  121.4 23.3 %all-gather.15.cloned.1.call-done = bf16[1,1,1536,3072]{3,2,1,0:T(8,128)(2,1)} async-done(((bf16[1,1,96,3072]{3,2,1,0:T(8,128)(2,1)}), bf16[1,1,1536,3072]{3,2,1,0:T(8,128)(2,1)}) %all-gather.15.cloned.1.call-update) | async-done | bytes 9437200 | tf_op jit(solution)/shard_map/all_gather | solution.py:179
  144.7 30.2 %convolution_convert_fusion.2 = bf16[4608,3072]{1,0:T(8,128)(2,1)} fusion(bf16[1,1,1536,3072]{3,2,1,0:T(8,128)(2,1)} %all-gather.15.cloned.1.call-done, bf16[4608,768]{1,0:T(8,128)(2,1)} %get-tuple-element.6, f32[4608]{0:T(1024)S(1)} %fusion.54), kind=kOutput, calls=%fused_computation.32 | convolution fusion | flops 21768044544 | bytes 40126464 | tf_op jit(solution)/shard_map/dot_general | solution.py:31
  174.9 24.5 %all-gather.11.cloned.1.call-done = bf16[1,1,6144,768]{3,2,1,0:T(8,128)(2,1)} async-done(((bf16[1,1,384,768]{3,2,1,0:T(8,128)(2,1)}), bf16[1,1,6144,768]{3,2,1,0:T(8,128)(2,1)}) %all-gather.11.cloned.1.call-update) | async-done | bytes 9437200 | tf_op jit(solution)/shard_map/all_gather | solution.py:179
  199.5 40.9 %fusion.30 = (f32[4608]{0:T(1024)S(1)}, bf16[4608,768]{1,0:T(8,128)(2,1)S(1)}) fusion(bf16[1,1,6144,768]{3,2,1,0:T(8,128)(2,1)} %all-gather.11.cloned.1.call-done, bf16[4608,3072]{1,0:T(8,128)(2,1)} %convolution_convert_fusion.2, bf16[4608,768]{1,0:T(8,128)(2,1)} %get-tuple-element.6), kind=kOutput, calls=%fused_computation.62 | convolution fusion | flops 21906059264 | bytes 47204352 | tf_op jit(solution)/shard_map/dot_general | solution.py:31
  241.0 24.2 %convolution_convert_fusion.1 = bf16[4608,2304]{1,0:T(8,128)(2,1)} fusion(bf16[1,1,1536,2304]{3,2,1,0:T(8,128)(2,1)} %all-gather.9.cloned.1.call-done, bf16[4608,768]{1,0:T(8,128)(2,1)S(1)} %get-tuple-element.8, f32[4608]{0:T(1024)S(1)} %fusion.55), kind=kOutput, calls=%fused_computation.31 | convolution fusion | flops 16328687616 | bytes 31868928 | tf_op jit(solution)/shard_map/dot_general | solution.py:31
  265.2 28.2 %attn_fwd.3 = bf16[36,128,768]{2,1,0:T(8,128)(2,1)} custom-call(bf16[36,128,2304]{2,1,0:T(8,128)(2,1)} %bitcast.99), custom_call_target="tpu_custom_call" | custom-call | flops 3623878656 | bytes 28311552 | tf_op jit(solution)/shard_map/attn_fwd/pallas_call | solution.py:100
  293.4 11.9 fusion.34
  305.3 30.3 %convolution_convert_fusion = bf16[4608,3072]{1,0:T(8,128)(2,1)} fusion(bf16[1,1,1536,3072]{3,2,1,0:T(8,128)(2,1)} %all-gather.15.cloned.1.call-done, bf16[4608,768]{1,0:T(8,128)(2,1)} %get-tuple-element.10, f32[4608]{0:T(1024)S(1)} %fusion.56), kind=kOutput, calls=%fused_computation.30 | convolution fusion | flops 21768044544 | bytes 40126464 | tf_op jit(solution)/shard_map/dot_general | solution.py:31
  335.6 64.2 %fusion.4 = bf16[4608,3072]{1,0:T(8,128)(2,1)} fusion(bf16[4608,3072]{1,0:T(8,128)(2,1)} %convolution_convert_fusion, bf16[4608,768]{1,0:T(8,128)(2,1)} %bitcast.101, bf16[1,1,6144,768]{3,2,1,0:T(8,128)(2,1)} %all-gather.11.cloned.1.call-done), kind=kOutput, calls=%fused_computation.14 | convolution fusion | flops 22040543232 | bytes 68419584 | tf_op jit(solution)/shard_map/dot_general | solution.py:35
  399.9 30.7 %fusion.36 = (f32[4608]{0:T(1024)S(1)}, f32[4608,768]{1,0:T(8,128)}) fusion(bf16[4608,768]{1,0:T(8,128)(2,1)} %get-tuple-element.10, bf16[4608,3072]{1,0:T(8,128)(2,1)} %fusion.4, bf16[1,1,1536,3072]{3,2,1,0:T(8,128)(2,1)} %all-gather.15.cloned.1.call-done), kind=kOutput, calls=%fused_computation.68 | convolution fusion | flops 21753884672 | bytes 54282240 | tf_op jit(solution)/shard_map/dot_general | solution.py:35
  430.7 8.9 fusion.21
  439.6 2.9 copy-done.4
  442.5 7.5 fusion.65
  450.1 10.8 convolution_convert_fusion.5
  460.9 68.4 %attn_bwd.2 = bf16[36,128,2304]{2,1,0:T(8,128)(2,1)} custom-call(bf16[36,128,2304]{2,1,0:T(8,128)(2,1)} %bitcast.100, bf16[36,128,768]{2,1,0:T(8,128)(2,1)} %bitcast.112), custom_call_target="tpu_custom_call" | custom-call | flops 9059696640 | bytes 49545216 | tf_op jit(solution)/shard_map/attn_bwd/pallas_call | solution.py:116
  529.4 24.4 %fusion.33 = (f32[4608]{0:T(1024)S(1)}, f32[4608,768]{1,0:T(8,128)}) fusion(bf16[4608,768]{1,0:T(8,128)(2,1)} %copy-done.7, bf16[4608,2304]{1,0:T(8,128)(2,1)} %bitcast.103, bf16[1,1,1536,2304]{3,2,1,0:T(8,128)(2,1)} %all-gather.9.cloned.1.call-done), kind=kOutput, calls=%fused_computation.65 | convolution fusion | flops 16318066688 | bytes 46024704 | tf_op jit(solution)/shard_map/dot_general | solution.py:35
  553.8 10.3 fusion.23
  564.1 64.5 %fusion.7 = bf16[4608,3072]{1,0:T(8,128)(2,1)} fusion(bf16[4608,3072]{1,0:T(8,128)(2,1)} %convolution_convert_fusion.2, bf16[4608,768]{1,0:T(8,128)(2,1)S(1)} %fusion.23, bf16[1,1,6144,768]{3,2,1,0:T(8,128)(2,1)} %all-gather.11.cloned.1.call-done), kind=kOutput, calls=%fused_computation.17 | convolution fusion | flops 22040543232 | bytes 68419584 | tf_op jit(solution)/shard_map/dot_general | solution.py:35
  628.6 30.6 %fusion.29 = (f32[4608]{0:T(1024)S(1)}, f32[4608,768]{1,0:T(8,128)}) fusion(bf16[4608,768]{1,0:T(8,128)(2,1)} %get-tuple-element.6, bf16[4608,3072]{1,0:T(8,128)(2,1)} %fusion.7, bf16[1,1,1536,3072]{3,2,1,0:T(8,128)(2,1)} %all-gather.15.cloned.1.call-done), kind=kOutput, calls=%fused_computation.61 | convolution fusion | flops 21753884672 | bytes 54282240 | tf_op jit(solution)/shard_map/dot_general | solution.py:35
  659.2 8.9 fusion.25
  668.1 2.9 copy-done.8
  671.0 7.7 fusion.64
  678.8 24.8 %fusion.48 = f32[768,2304]{1,0:T(8,128)} fusion(bf16[4608,2304]{1,0:T(8,128)(2,1)} %bitcast.104, bf16[4608,768]{1,0:T(8,128)(2,1)} %copy-done.7, f32[4608]{0:T(1024)S(1)} %copy-done.19), kind=kOutput, calls=%fused_computation.91 | convolution fusion | flops 16318070784 | bytes 35407872 | tf_op jit(solution)/shard_map/dot_general | solution.py:39
  703.6 7.3 fusion.39
  711.0 10.9 convolution_convert_fusion.4
  721.9 68.4 %attn_bwd.3 = bf16[36,128,2304]{2,1,0:T(8,128)(2,1)} custom-call(bf16[36,128,2304]{2,1,0:T(8,128)(2,1)} %bitcast.98, bf16[36,128,768]{2,1,0:T(8,128)(2,1)} %bitcast.111), custom_call_target="tpu_custom_call" | custom-call | flops 9059696640 | bytes 49545216 | tf_op jit(solution)/shard_map/attn_bwd/pallas_call | solution.py:116
  790.4 23.9 %fusion.63 = f32[768,2304]{1,0:T(8,128)} fusion(bf16[4608,768]{1,0:T(8,128)(2,1)} %bitcast.110, bf16[4608,2304]{1,0:T(8,128)(2,1)} %bitcast.105), kind=kOutput, calls=%fused_computation.117 | convolution fusion | flops 16307453952 | bytes 35389440 | tf_op jit(solution)/shard_map/dot_general | solution.py:39
  814.4 37.8 %fusion.58 = f32[3072,768]{1,0:T(8,128)} fusion(bf16[4608,768]{1,0:T(8,128)(2,1)} %bitcast.102, bf16[4608,3072]{1,0:T(8,128)(2,1)} %convolution_convert_fusion), kind=kOutput, calls=%fused_computation.115 | convolution fusion | flops 21884829696 | bytes 44826624 | tf_op jit(solution)/shard_map/dot_general | solution.py:39
  852.2 37.1 %fusion.60 = f32[3072,768]{1,0:T(8,128)} fusion(bf16[4608,768]{1,0:T(8,128)(2,1)} %copy-done.3, bf16[4608,3072]{1,0:T(8,128)(2,1)} %convolution_convert_fusion.2), kind=kOutput, calls=%fused_computation.116 | convolution fusion | flops 21884829696 | bytes 44826624 | tf_op jit(solution)/shard_map/dot_general | solution.py:39
  889.4 30.8 %fusion.45 = f32[768,3072]{1,0:T(8,128)} fusion(bf16[4608,3072]{1,0:T(8,128)(2,1)} %fusion.4, bf16[4608,768]{1,0:T(8,128)(2,1)} %get-tuple-element.10, f32[4608]{0:T(1024)S(1)} %copy-done.16), kind=kOutput, calls=%fused_computation.90 | convolution fusion | flops 21753888768 | bytes 44845056 | tf_op jit(solution)/shard_map/dot_general | solution.py:39
  920.3 30.7 %fusion.51 = f32[768,3072]{1,0:T(8,128)} fusion(bf16[4608,3072]{1,0:T(8,128)(2,1)} %fusion.7, bf16[4608,768]{1,0:T(8,128)(2,1)} %get-tuple-element.6, f32[4608]{0:T(1024)S(1)} %copy-done.13), kind=kOutput, calls=%fused_computation.92 | convolution fusion | flops 21753888768 | bytes 44845056 | tf_op jit(solution)/shard_map/dot_general | solution.py:39
  951.0 41.3 %fusion.37 = bf16[4608,768]{1,0:T(8,128)(2,1)} fusion(bf16[4608,768]{1,0:T(8,128)(2,1)} %get-tuple-element.10, bf16[1,1,6144,768]{3,2,1,0:T(8,128)(2,1)} %all-gather.11.cloned.1.call-done, bf16[4608,3072]{1,0:T(8,128)(2,1)} %convolution_convert_fusion), kind=kOutput, calls=%fused_computation.69 | convolution fusion | flops 21895446528 | bytes 47185920 | tf_op jit(solution)/shard_map/dot_general | solution.py:31
  992.3 1.2 collective-permute-start.8
  993.5 2.7 collective-permute-start.3
  996.3 1.3 collective-permute-start.2
  997.6 154.3 %collective-permute-done.3 = f32[96,768]{1,0:T(8,128)S(1)} collective-permute-done((f32[96,768]{1,0:T(8,128)}, f32[96,768]{1,0:T(8,128)S(1)}, u32[]{:S(2)}, u32[]{:S(2)}) %collective-permute-start.3) | collective-permute-done | bytes 294944 | tf_op jit(solution)/shard_map/ppermute | solution.py:203
  1151.9 1.3 collective-permute-done.2
  1153.1 1.8 select_bitcast_fusion.3
  1155.0 4.1 collective-permute-start.1
  1159.0 1.3 collective-permute-start
  1160.4 6.5 collective-permute-start.7
  1166.9 1.3 collective-permute-start.6
  1168.2 15.8 %maximum_select_fusion = bf16[12,6,128,768]{3,2,1,0:T(8,128)(2,1)} fusion(bf16[6,6,128,768]{3,2,1,0:T(8,128)(2,1)} %collective-permute-done.8, bf16[6,6,128,768]{3,2,1,0:T(8,128)(2,1)} %bitcast.23, pred[]{:T(512)S(6)} %eq.3), kind=kLoop, calls=%fused_computation.70 | loop fusion | flops 21233664 | bytes 28311552 | tf_op jit(solution)/shard_map/jit(_where)/select_n | solution.py:194
  1184.0 6.6 collective-permute-start.5
  1190.5 1.3 collective-permute-start.4
  1191.8 3.0 select_bitcast_fusion.2
  1194.9 8.5 collective-permute-done.7
  1203.4 5.4 collective-permute-done.6
  1208.7 3.6 select_bitcast_fusion
  1212.4 14.7 %collective-permute-done.5 = f32[96,3072]{1,0:T(8,128)} collective-permute-done((f32[96,3072]{1,0:T(8,128)}, f32[96,3072]{1,0:T(8,128)}, u32[]{:S(2)}, u32[]{:S(2)}) %collective-permute-start.5) | collective-permute-done | bytes 1179680 | tf_op jit(solution)/shard_map/ppermute | solution.py:203
  1227.1 5.1 collective-permute-done.4
  1232.2 3.3 select_bitcast_fusion.1
  (100 shorter events, 2.4 us)
Async XLA Ops:
  7.2 2.0 copy-start
  7.2 50.8 %all-gather.9.cloned.1.call-start = ((), (), s32[]{:S(2)}) async-start(), calls=%async_computation.16 | async-start | bytes 7520256 | tf_op jit(solution)/shard_map/all_gather | solution.py:179
  10.0 99.6 %all-gather.13.cloned.1.call-start = ((), (), s32[]{:S(2)}) async-start(), calls=%async_computation.18 | async-start | bytes 2506752 | tf_op jit(solution)/shard_map/all_gather | solution.py:179
  11.7 133.1 %all-gather.15.cloned.1.call-start = ((), (), s32[]{:S(2)}) async-start(), calls=%async_computation.19 | async-start | bytes 10027008 | tf_op jit(solution)/shard_map/all_gather | solution.py:179
  13.7 185.8 %all-gather.11.cloned.1.call-start = ((), (), s32[]{:S(2)}) async-start(), calls=%async_computation.17 | async-start | bytes 10027008 | tf_op jit(solution)/shard_map/all_gather | solution.py:179
  15.7 977.9 %reduce-scatter.15.cloned.1.call-start = ((), (), s32[]{:S(2)}) async-start(), calls=%async_computation.11 | async-start | bytes 2654208 | tf_op jit(solution)/shard_map/reduce_scatter | solution.py:185
  20.2 13.3 %copy-start.9 = (f32[6,6,128]{2,1,0:T(8,128)}, f32[6,6,128]{2,1,0:T(8,128)S(1)}, u32[]{:S(2)}) copy-start(f32[6,6,128]{2,1,0:T(8,128)S(1)} %add_rsqrt_fusion) | copy-start | bytes 55300
  121.4 53.5 %copy-start.20 = (f32[4608]{0:T(1024)}, f32[4608]{0:T(1024)S(1)}, u32[]{:S(2)}) copy-start(f32[4608]{0:T(1024)S(1)} %get-tuple-element.5) | copy-start | bytes 55300
  121.4 53.5 %copy-start.11 = (f32[4608]{0:T(1024)}, f32[4608]{0:T(1024)S(1)}, u32[]{:S(2)}) copy-start(f32[4608]{0:T(1024)S(1)} %fusion.54) | copy-start | bytes 55300
  240.3 0.6 copy-start.22
  240.4 24.9 %copy-start.7 = (bf16[4608,768]{1,0:T(8,128)(2,1)}, bf16[4608,768]{1,0:T(8,128)(2,1)S(1)}, u32[]{:S(2)}) copy-start(bf16[4608,768]{1,0:T(8,128)(2,1)S(1)} %get-tuple-element.8) | copy-start | bytes 21233668
  241.0 24.2 %copy-start.17 = (f32[4608]{0:T(1024)}, f32[4608]{0:T(1024)S(1)}, u32[]{:S(2)}) copy-start(f32[4608]{0:T(1024)S(1)} %fusion.55) | copy-start | bytes 55300
  265.2 28.2 %copy-start.26 = (bf16[1,1,1536,768]{3,2,1,0:T(8,128)(2,1)S(1)}, bf16[1,1,1536,768]{3,2,1,0:T(8,128)(2,1)}, u32[]{:S(2)}) copy-start(bf16[1,1,1536,768]{3,2,1,0:T(8,128)(2,1)} %all-gather.13.cloned.1.call-done) | copy-start | bytes 7077892
  305.3 30.3 %copy-start.24 = (f32[4608]{0:T(1024)}, f32[4608]{0:T(1024)S(1)}, u32[]{:S(2)}) copy-start(f32[4608]{0:T(1024)S(1)} %get-tuple-element.9) | copy-start | bytes 55300
  305.3 30.3 %copy-start.14 = (f32[4608]{0:T(1024)}, f32[4608]{0:T(1024)S(1)}, u32[]{:S(2)}) copy-start(f32[4608]{0:T(1024)S(1)} %fusion.56) | copy-start | bytes 55300
  399.9 30.8 %copy-start.25 = (f32[4608]{0:T(1024)S(1)}, f32[4608]{0:T(1024)}, u32[]{:S(2)}) copy-start(f32[4608]{0:T(1024)} %copy-done.24) | copy-start | bytes 55300
  399.9 30.8 %copy-start.2 = (bf16[6,6,128,768]{3,2,1,0:T(8,128)(2,1)S(1)}, bf16[6,6,128,768]{3,2,1,0:T(8,128)(2,1)}, u32[]{:S(2)}) copy-start(bf16[6,6,128,768]{3,2,1,0:T(8,128)(2,1)} %constant_dynamic-slice_fusion.3) | copy-start | bytes 21233668
  399.9 30.8 %copy-start.15 = (f32[4608]{0:T(1024)S(1)}, f32[4608]{0:T(1024)}, u32[]{:S(2)}) copy-start(f32[4608]{0:T(1024)} %copy-done.14) | copy-start | bytes 55300
  430.7 11.9 copy-start.6
  439.6 2.9 copy-start.4
  442.5 7.6 copy-start.27
  450.1 546.2 %reduce-scatter.13.cloned.1.call-start = ((), (), s32[]{:S(2)}) async-start(), calls=%async_computation.10 | async-start | bytes 2654208 | tf_op jit(solution)/shard_map/reduce_scatter | solution.py:185
  529.4 24.4 %copy-start.23 = (f32[4608]{0:T(1024)S(1)}, f32[4608]{0:T(1024)}, u32[]{:S(2)}) copy-start(f32[4608]{0:T(1024)} %copy-done.22) | copy-start | bytes 55300
  529.4 24.4 %copy-start.18 = (f32[4608]{0:T(1024)S(1)}, f32[4608]{0:T(1024)}, u32[]{:S(2)}) copy-start(f32[4608]{0:T(1024)} %copy-done.17) | copy-start | bytes 55300
  564.1 95.0 %copy-start.3 = (bf16[4608,768]{1,0:T(8,128)(2,1)}, bf16[4608,768]{1,0:T(8,128)(2,1)S(1)}, u32[]{:S(2)}) copy-start(bf16[4608,768]{1,0:T(8,128)(2,1)S(1)} %fusion.23) | copy-start | bytes 21233668
  628.6 30.6 %copy-start.21 = (f32[4608]{0:T(1024)S(1)}, f32[4608]{0:T(1024)}, u32[]{:S(2)}) copy-start(f32[4608]{0:T(1024)} %copy-done.20) | copy-start | bytes 55300
  628.6 30.6 %copy-start.12 = (f32[4608]{0:T(1024)S(1)}, f32[4608]{0:T(1024)}, u32[]{:S(2)}) copy-start(f32[4608]{0:T(1024)} %copy-done.11) | copy-start | bytes 55300
  659.2 11.9 copy-start.5
  668.1 2.9 copy-start.8
  671.0 7.8 copy-start.19
  678.7 24.9 %copy-start.10 = (f32[6,6,128]{2,1,0:T(8,128)S(1)}, f32[6,6,128]{2,1,0:T(8,128)}, u32[]{:S(2)}) copy-start(f32[6,6,128]{2,1,0:T(8,128)} %copy-done.9) | copy-start | bytes 55300
  678.7 476.2 %reduce-scatter.11.cloned.1.call-start = ((), (), s32[]{:S(2)}) async-start(), calls=%async_computation.9 | async-start | bytes 7962624 | tf_op jit(solution)/shard_map/reduce_scatter | solution.py:185
  703.6 7.4 copy-start.28
  703.6 455.5 %reduce-scatter.9.cloned.1.call-start = ((), (), s32[]{:S(2)}) async-start(), calls=%async_computation.8 | async-start | bytes 7962624 | tf_op jit(solution)/shard_map/reduce_scatter | solution.py:185
  814.3 346.0 %reduce-scatter.23.cloned.1.call-start = ((), (), s32[]{:S(2)}) async-start(), calls=%async_computation.15 | async-start | bytes 10616832 | tf_op jit(solution)/shard_map/reduce_scatter | solution.py:185
  852.1 37.3 %copy-start.16 = (f32[4608]{0:T(1024)S(1)}, f32[4608]{0:T(1024)}, u32[]{:S(2)}) copy-start(f32[4608]{0:T(1024)} %copy-done.14) | copy-start | bytes 55300
  852.2 314.7 %reduce-scatter.21.cloned.1.call-start = ((), (), s32[]{:S(2)}) async-start(), calls=%async_computation.14 | async-start | bytes 10616832 | tf_op jit(solution)/shard_map/reduce_scatter | solution.py:185
  889.4 30.9 %copy-start.13 = (f32[4608]{0:T(1024)S(1)}, f32[4608]{0:T(1024)}, u32[]{:S(2)}) copy-start(f32[4608]{0:T(1024)} %copy-done.11) | copy-start | bytes 55300
  889.4 294.6 %reduce-scatter.19.cloned.1.call-start = ((), (), s32[]{:S(2)}) async-start(), calls=%async_computation.13 | async-start | bytes 10616832 | tf_op jit(solution)/shard_map/reduce_scatter | solution.py:185
  920.2 270.3 %reduce-scatter.17.cloned.1.call-start = ((), (), s32[]{:S(2)}) async-start(), calls=%async_computation.12 | async-start | bytes 10616832 | tf_op jit(solution)/shard_map/reduce_scatter | solution.py:185
  992.3 175.8 %collective-permute-start.8 = (bf16[6,6,128,768]{3,2,1,0:T(8,128)(2,1)}, bf16[6,6,128,768]{3,2,1,0:T(8,128)(2,1)}, u32[]{:S(2)}, u32[]{:S(2)}) collective-permute-start(bf16[6,6,128,768]{3,2,1,0:T(8,128)(2,1)} %bitcast.23), channel_id=1, source_target_pairs={{0,8},{8,0},{1,9},{9,1},{2,10},{10,2},{3,11},{11,3},{4,12},{12,4},... | collective-permute-start | bytes 21233672 | tf_op jit(solution)/shard_map/ppermute | solution.py:193
  993.5 158.3 %collective-permute-start.3 = (f32[96,768]{1,0:T(8,128)}, f32[96,768]{1,0:T(8,128)S(1)}, u32[]{:S(2)}, u32[]{:S(2)}) collective-permute-start(f32[96,768]{1,0:T(8,128)} %reduce-scatter.15.cloned.1.call-done), channel_id=1, source_target_pairs={{0,8},{1,9},{2,10},{3,11},{4,12},{5,13},{6,14},{7,15}} | collective-permute-start | bytes 884744 | tf_op jit(solution)/shard_map/ppermute | solution.py:203
  996.3 156.9 %collective-permute-start.2 = (f32[96,768]{1,0:T(8,128)}, f32[96,768]{1,0:T(8,128)S(1)}, u32[]{:S(2)}, u32[]{:S(2)}) collective-permute-start(f32[96,768]{1,0:T(8,128)} %reduce-scatter.13.cloned.1.call-done), channel_id=1, source_target_pairs={{8,0},{9,1},{10,2},{11,3},{12,4},{13,5},{14,6},{15,7}} | collective-permute-start | bytes 884744 | tf_op jit(solution)/shard_map/ppermute | solution.py:204
  1155.0 35.6 %collective-permute-start.1 = (f32[96,2304]{1,0:T(8,128)}, f32[96,2304]{1,0:T(8,128)}, u32[]{:S(2)}, u32[]{:S(2)}) collective-permute-start(f32[96,2304]{1,0:T(8,128)} %reduce-scatter.11.cloned.1.call-done), channel_id=1, source_target_pairs={{0,8},{1,9},{2,10},{3,11},{4,12},{5,13},{6,14},{7,15}} | collective-permute-start | bytes 2654216 | tf_op jit(solution)/shard_map/ppermute | solution.py:203
  1159.0 32.8 %collective-permute-start = (f32[96,2304]{1,0:T(8,128)}, f32[96,2304]{1,0:T(8,128)}, u32[]{:S(2)}, u32[]{:S(2)}) collective-permute-start(f32[96,2304]{1,0:T(8,128)} %reduce-scatter.9.cloned.1.call-done), channel_id=1, source_target_pairs={{8,0},{9,1},{10,2},{11,3},{12,4},{13,5},{14,6},{15,7}} | collective-permute-start | bytes 2654216 | tf_op jit(solution)/shard_map/ppermute | solution.py:204
  1160.4 43.0 %collective-permute-start.7 = (f32[384,768]{1,0:T(8,128)}, f32[384,768]{1,0:T(8,128)}, u32[]{:S(2)}, u32[]{:S(2)}) collective-permute-start(f32[384,768]{1,0:T(8,128)} %reduce-scatter.23.cloned.1.call-done), channel_id=1, source_target_pairs={{0,8},{1,9},{2,10},{3,11},{4,12},{5,13},{6,14},{7,15}} | collective-permute-start | bytes 3538952 | tf_op jit(solution)/shard_map/ppermute | solution.py:203
  1166.9 41.9 %collective-permute-start.6 = (f32[384,768]{1,0:T(8,128)}, f32[384,768]{1,0:T(8,128)}, u32[]{:S(2)}, u32[]{:S(2)}) collective-permute-start(f32[384,768]{1,0:T(8,128)} %reduce-scatter.21.cloned.1.call-done), channel_id=1, source_target_pairs={{8,0},{9,1},{10,2},{11,3},{12,4},{13,5},{14,6},{15,7}} | collective-permute-start | bytes 3538952 | tf_op jit(solution)/shard_map/ppermute | solution.py:204
  1168.2 67.3 %copy-start.1 = (bf16[1,1,768,2304]{3,2,1,0:T(8,128)(2,1)S(1)}, bf16[1,1,768,2304]{3,2,1,0:T(8,128)(2,1)}, u32[]{:S(2)}) copy-start(bf16[1,1,768,2304]{3,2,1,0:T(8,128)(2,1)} %param.8) | copy-start | bytes 10616836
  1184.0 43.1 %collective-permute-start.5 = (f32[96,3072]{1,0:T(8,128)}, f32[96,3072]{1,0:T(8,128)}, u32[]{:S(2)}, u32[]{:S(2)}) collective-permute-start(f32[96,3072]{1,0:T(8,128)} %reduce-scatter.19.cloned.1.call-done), channel_id=1, source_target_pairs={{0,8},{1,9},{2,10},{3,11},{4,12},{5,13},{6,14},{7,15}} | collective-permute-start | bytes 3538952 | tf_op jit(solution)/shard_map/ppermute | solution.py:203
  1190.5 41.6 %collective-permute-start.4 = (f32[96,3072]{1,0:T(8,128)}, f32[96,3072]{1,0:T(8,128)S(1)}, u32[]{:S(2)}, u32[]{:S(2)}) collective-permute-start(f32[96,3072]{1,0:T(8,128)} %reduce-scatter.17.cloned.1.call-done), channel_id=1, source_target_pairs={{8,0},{9,1},{10,2},{11,3},{12,4},{13,5},{14,6},{15,7}} | collective-permute-start | bytes 3538952 | tf_op jit(solution)/shard_map/ppermute | solution.py:204
Sparse Core Ops, SparseCore 0:
  10.8 47.1 all-gather.8
  60.8 28.9 all-gather.12
  92.6 52.0 all-gather.14
  147.4 52.0 all-gather.10
  450.2 36.5 reduce-scatter.14
  678.9 36.5 reduce-scatter.12
  718.9 59.1 reduce-scatter.10
  814.4 59.1 reduce-scatter.8
  877.7 70.1 reduce-scatter.22
  951.1 70.1 reduce-scatter.20
  1024.8 70.1 reduce-scatter.18
  1098.3 70.1 reduce-scatter.16
